TPU v7x, 256 devices: a whole 4x4x8 slice. The times are simulated.
256 devices in a mesh: hi: 8 (over y, core), lo: 32 (over z, x).
Axes of the slice: x: 4, y: 4, z: 8, core: 2. Of those that a mesh axis runs over, the one named last changes fastest.
Arguments:
- grm: bfloat16 [8, 32, 64, 8, 2048], P(None, 'lo', None, 'hi'), as said below
- right_sides: float32 [16384, 512], P(('hi', 'lo')), may hold values from -6 to 6
- inv_diag: float32 [16384], P(('hi', 'lo')), may hold values from 0.3 to 1
- bases: float32 [16384, 576], P(('hi', 'lo')), may hold values from -0.75 to 0.75
- couplings: float32 [9, 64, 64], replicated, as said below
- level_map: int32 [8], replicated, may hold values from 0 to 7, each once
- variance: float32 [2], replicated, may hold values from 0.3 to 1.5
- iters_per_column: int32 [512], replicated, may hold values from 1 to 3
Outputs:
- solution: float32 [16384, 512], P(('hi', 'lo'))
- residual: float32 [16384, 512], P(('hi', 'lo'))
Inputs may be any that keep to these rules, and one draw needn't show every extreme that they name: `grm`: G is symmetric and positive definite. `couplings`: each of the 9 matrices is symmetric and positive definite. `level_map`: a permutation of the levels.
All inputs are finite; a program needn't handle non-finite values.
Results may differ from a plain program's by a relative error of at most 0.0055.
Values may be sent and summed in bfloat16 or wider, within the bound.
A program may use at most 64 MiB of HBM per device.

v0:
```python
import jax
import jax.numpy as jnp
from jax import lax
from jax.sharding import Mesh
from jax.sharding import PartitionSpec as P

ITERS = 3
LO = ("lo_0", "lo_1")
HI = ("hi_0", "hi_1")
HI_LO = ("hi_0", "hi_1", "lo_0", "lo_1")


def gather_axes(array, axes, dim):
    if not axes:
        return array
    nearer = lax.all_gather(array, axes[-1], axis=dim, tiled=True)
    return gather_axes(nearer, axes[:-1], dim)


def split_up(array, dim, length):
    shape = array.shape
    tiles = array.reshape(*shape[:dim], length, shape[dim] // length, *shape[dim + 1 :])
    return jnp.moveaxis(tiles, dim, 0)


def sent_and_summed(array, axis, dim):
    tiles = split_up(array, dim, lax.axis_size(axis))
    arrived = lax.all_to_all(tiles, axis, split_axis=0, concat_axis=0, tiled=True)
    return arrived.sum(axis=0)


def from_partner(value, axis, bit):
    mask = 2**bit
    pairs = [(source, source ^ mask) for source in range(lax.axis_size(axis))]
    return lax.ppermute(value, axis, pairs)


def sum_by_axis(array, axes, dim):
    far, near = axes
    tiles = split_up(array, dim, lax.axis_size(far))
    nearer = sent_and_summed(tiles, near, dim + 1)
    arrived = lax.all_to_all(nearer, far, split_axis=0, concat_axis=0, tiled=True)
    return arrived.sum(axis=0)


def padded_to(lines, length):
    spare = -lines.shape[0] % length
    if not spare:
        return lines
    return jnp.concatenate([lines, jnp.zeros((spare, *lines.shape[1:]), lines.dtype)])


def from_everyone(array, axis):
    copies = jnp.broadcast_to(array, (lax.axis_size(axis), *array.shape))
    return lax.all_to_all(copies, axis, split_axis=0, concat_axis=0, tiled=True)


def laid_out(tiles, dim):
    shape = list(tiles.shape[1:])
    shape[dim] *= tiles.shape[0]
    return jnp.moveaxis(tiles, 0, dim).reshape(shape)


def gathered_by_axis(array, axes, dim):
    far, near = axes
    first = from_everyone(array, far)
    tiles = jnp.swapaxes(from_everyone(first, near), 0, 1)
    return laid_out(tiles.reshape(-1, *array.shape), dim)


def total_of(array, axes):
    own = sum_by_axis(padded_to(array, lax.axis_size(axes[0]) * lax.axis_size(axes[1])), axes, 0)
    whole = gathered_by_axis(own, axes, 0)
    return whole[: len(array)].reshape(array.shape)


def together(arrays, axis):
    flat, at, done = (jnp.concatenate([a.reshape(-1) for a in arrays]), 0, [])
    total = total_of(flat, axis)
    for a in arrays:
        done.append(total[at : at + a.size].reshape(a.shape))
        at += a.size
    return tuple(done)


def of_everyone(array, axis):
    return from_everyone(array, axis).sum(axis=0)


def by_axis(array, axes):
    far, near = axes
    nearer = of_everyone(array, near)
    return of_everyone(nearer, far)


def level_pieces(coefficients, couplings, level):
    level_ids = jnp.arange(couplings.shape[0], dtype=jnp.int32)
    select = (level_ids == level).astype(jnp.float32)
    own_part = jnp.einsum("l,lrb->rb", select, coefficients)
    matrix = jnp.einsum("l,lrs->rs", select, couplings)
    return (own_part, matrix, select)


def add_level(stacked, own_part, other_part, matrix, select):
    term = jnp.dot(matrix, own_part + other_part, precision=lax.Precision.HIGHEST)
    return stacked + select[:, None, None] * term[None]


def local(grm, right_sides, inv_diag, bases, couplings, level_map, variance, iters_per_column):
    row_count, column_count = right_sides.shape
    grm_block = grm.reshape(-1, grm.shape[4])
    level_total = couplings.shape[0]
    rank_width = couplings.shape[1]
    lo_bits = lax.axis_size(LO).bit_length() - 1
    hi_bits = lax.axis_size(HI).bit_length() - 1
    genetic = variance[0]
    noise = variance[1]

    def precondition(resid):
        coefficients = lax.dot_general(
            bases, resid, (((0,), (0,)), ((), ())), precision=lax.Precision.HIGHEST
        )
        coefficients = coefficients.reshape(level_total, rank_width, column_count)
        stacked = jnp.zeros((level_total - 1, rank_width, column_count), jnp.float32)
        for bit_index in range(lo_bits):
            own_part, matrix, select = level_pieces(coefficients, couplings, level_map[bit_index])
            other_part = from_partner(own_part.astype(jnp.bfloat16), LO, bit_index).astype(
                own_part.dtype
            )
            stacked = add_level(stacked, own_part, other_part, matrix, select[: level_total - 1])
        for bit_index in range(hi_bits):
            own_part, matrix, select = level_pieces(
                coefficients, couplings, level_map[lo_bits + bit_index]
            )
            other_part = from_partner(own_part.astype(jnp.bfloat16), HI, bit_index).astype(
                own_part.dtype
            )
            stacked = add_level(stacked, own_part, other_part, matrix, select[: level_total - 1])
        split_at = (level_total - 1) * rank_width
        local_part = inv_diag[:, None] * resid + jnp.dot(
            bases[:, :split_at],
            stacked.reshape(split_at, column_count),
            precision=lax.Precision.HIGHEST,
        )
        coarse_basis = bases[:, split_at:]
        partial_energy = jnp.sum(resid * local_part, axis=0)
        total, summed_energy = together(
            (coefficients[level_total - 1], partial_energy), (("hi_0", "hi_1", "lo_0"), "lo_1")
        )
        coarse = jnp.dot(couplings[level_total - 1], total, precision=lax.Precision.HIGHEST)
        scaled = local_part + jnp.dot(coarse_basis, coarse, precision=lax.Precision.HIGHEST)
        energy = summed_energy + jnp.sum(total * coarse, axis=0)
        return (scaled, energy)

    solution = jnp.zeros_like(right_sides)
    residual = right_sides
    scaled, energy = precondition(residual)
    direction = scaled
    for step in range(ITERS):
        rounded = direction.astype(jnp.bfloat16)
        partial_value = jnp.dot(
            grm_block, gather_axes(rounded, LO, 0), preferred_element_type=jnp.float32
        )
        product = sent_and_summed(partial_value, HI, 0)
        image = genetic * product + noise * direction
        curvature = by_axis(jnp.sum(direction * image, axis=0), ("hi_0", ("hi_1", "lo_0", "lo_1")))
        alpha = energy / curvature
        stepsize = jnp.where(step < iters_per_column, alpha, jnp.zeros_like(alpha))
        solution = solution + stepsize * direction
        residual = residual - stepsize * image
        if step + 1 < ITERS:
            scaled, fresh = precondition(residual)
            direction = scaled + fresh / energy * direction
            energy = fresh
    return (solution, residual)


def solution(mesh):
    split = Mesh(mesh.devices.reshape(4, 2, 8, 4), ("hi_0", "hi_1", "lo_0", "lo_1"))
    return jax.shard_map(
        local,
        mesh=split,
        in_specs=(
            P(None, LO, None, HI, None),
            P(HI_LO, None),
            P(HI_LO),
            P(HI_LO, None),
            P(),
            P(),
            P(),
            P(),
        ),
        out_specs=(P(HI_LO, None), P(HI_LO, None)),
        check_vma=False,
    )
```

profile of v0, /device:TPU:1, one launch (start us, length us, event | category | flops | bytes accessed | tf_op | source)
XLA Modules:
  0.0 613.6 jit_solution(17472519000649362641)
XLA Ops:
  7.2 1.6 fusion.221
  8.8 2.1 fusion.225
  12.9 3.6 collective-permute-start.1
  16.5 1.4 fusion.42
  18.5 1.6 collective-permute-start.2
  22.1 3.0 collective-permute-start.3
  25.1 1.4 fusion.38
  27.1 4.2 collective-permute-start.4
  31.4 1.4 fusion.36
  33.4 2.0 collective-permute-start.5
  40.1 1.6 fusion.60
  41.7 1.5 fusion.62
  43.2 1.5 fusion.64
  45.6 1.4 fusion.68
  49.3 1.5 fusion.58
  52.2 1.4 fusion.32
  73.6 1.4 collective-permute-start.6
  76.1 2.7 collective-permute-start.7
  86.8 8.3 %all_to_all.135 = f32[4,64,130]{2,1,0:T(8,128)S(1)} all-to-all(f32[4,64,130]{2,1,0:T(8,128)S(1)} %copy.31), channel_id=1, replica_groups=mesh['hi_0'=4,'hi_1'=2,'lo_0'=8,'lo_1'=4] {'lo_1'}, dimensions={0} | all-to-all | bytes 266240 | tf_op jit(solution)/shard_map/all_to_all | solution.py:28
  95.2 15.3 %all_to_all.136 = f32[64,1,130]{2,1,0:T(1,128)S(1)} all-to-all(f32[64,1,130]{2,1,0:T(1,128)S(1)} %all_to_all.88), channel_id=1, replica_groups=mesh['hi_0'=4,'hi_1'=2,'lo_0'=8,'lo_1'=4] {'hi_0','hi_1','lo_0'}, dimensions={0} | all-to-all | bytes 66560 | tf_op jit(solution)/shard_map/all_to_all | solution.py:42
  110.7 13.7 %all_to_all.137 = f32[64,1,130]{2,1,0:T(1,128)S(1)} all-to-all(f32[64,1,130]{2,1,0:T(1,128)S(1)} %broadcast_in_dim.24), channel_id=1, replica_groups=mesh['hi_0'=4,'hi_1'=2,'lo_0'=8,'lo_1'=4] {'hi_0','hi_1','lo_0'}, dimensions={0} | all-to-all | bytes 66560 | tf_op jit(solution)/shard_map/all_to_all | solution.py:55
  124.4 8.3 %all_to_all.138 = f32[4,64,130]{2,1,0:T(8,128)S(1)} all-to-all(f32[4,64,130]{2,1,0:T(8,128)S(1)} %broadcast_in_dim.25), channel_id=1, replica_groups=mesh['hi_0'=4,'hi_1'=2,'lo_0'=8,'lo_1'=4] {'lo_1'}, dimensions={0} | all-to-all | bytes 266240 | tf_op jit(solution)/shard_map/all_to_all | solution.py:55
  133.8 10.5 %all_gather.18 = bf16[256,512]{1,0:T(8,128)(2,1)} all-gather(bf16[64,512]{1,0:T(8,128)(2,1)S(1)} %get-tuple-element.16), channel_id=1, replica_groups=mesh['hi_0'=4,'hi_1'=2,'lo_0'=8,'lo_1'=4] {'lo_1'}, dimensions={0}, use_global_device_ids=true | all-gather | bytes 327680 | tf_op jit(solution)/shard_map/all_gather | solution.py:16
  144.4 34.5 %all-gather.4.cloned.1.call-done = bf16[2048,512]{1,0:T(8,128)(2,1)} async-done(((bf16[256,512]{1,0:T(8,128)(2,1)}), bf16[2048,512]{1,0:T(8,128)(2,1)}) %all-gather.4.cloned.1.call-update) | async-done | bytes 2097168 | tf_op jit(solution)/shard_map/all_gather | solution.py:16
  178.9 3.8 fusion.228
  182.7 9.3 %all-to-all-start.4 = ((f32[8,64,512]{2,1,0:T(8,128)}), f32[8,64,512]{2,1,0:T(8,128)}, u32[]{:S(2)}, u32[]{:S(2)}) async-start(f32[8,64,512]{2,1,0:T(8,128)} %bitcast.539), calls=%async_computation.4 | async-start | bytes 2097152 | tf_op jit(solution)/shard_map/all_to_all | solution.py:28
  192.6 14.5 %all-to-all-done.4 = f32[8,64,512]{2,1,0:T(8,128)} async-done(((f32[8,64,512]{2,1,0:T(8,128)}), f32[8,64,512]{2,1,0:T(8,128)}, u32[]{:S(2)}, u32[]{:S(2)}) %all-to-all-start.4) | async-done | bytes 1048608 | tf_op jit(solution)/shard_map/all_to_all | solution.py:28
  209.8 18.6 %all_to_all.139 = f32[64,1,512]{2,1,0:T(1,128)S(1)} all-to-all(f32[64,1,512]{2,1,0:T(1,128)S(1)} %broadcast_in_dim.26), channel_id=1, replica_groups=mesh['hi_0'=4,'hi_1'=2,'lo_0'=8,'lo_1'=4] {'hi_1','lo_0','lo_1'}, dimensions={0} | all-to-all | bytes 262144 | tf_op jit(solution)/shard_map/all_to_all | solution.py:55
  229.1 3.2 all-to-all-start.6
  232.7 3.8 all-to-all-done.6
  240.4 1.4 fusion.26
  244.5 1.4 fusion.20
  247.3 1.4 fusion.16
  252.9 3.0 collective-permute-start.12
  256.0 2.3 collective-permute-start.13
  259.1 1.9 collective-permute-start.15
  267.1 8.4 %all_to_all.140 = f32[4,64,130]{2,1,0:T(8,128)S(1)} all-to-all(f32[4,64,130]{2,1,0:T(8,128)S(1)} %copy.36), channel_id=1, replica_groups=mesh['hi_0'=4,'hi_1'=2,'lo_0'=8,'lo_1'=4] {'lo_1'}, dimensions={0} | all-to-all | bytes 266240 | tf_op jit(solution)/shard_map/all_to_all | solution.py:28
  275.5 19.0 %all_to_all.141 = f32[64,1,130]{2,1,0:T(1,128)S(1)} all-to-all(f32[64,1,130]{2,1,0:T(1,128)S(1)} %all_to_all.97), channel_id=1, replica_groups=mesh['hi_0'=4,'hi_1'=2,'lo_0'=8,'lo_1'=4] {'hi_0','hi_1','lo_0'}, dimensions={0} | all-to-all | bytes 66560 | tf_op jit(solution)/shard_map/all_to_all | solution.py:42
  294.6 13.7 %all_to_all.142 = f32[64,1,130]{2,1,0:T(1,128)S(1)} all-to-all(f32[64,1,130]{2,1,0:T(1,128)S(1)} %broadcast_in_dim.28), channel_id=1, replica_groups=mesh['hi_0'=4,'hi_1'=2,'lo_0'=8,'lo_1'=4] {'hi_0','hi_1','lo_0'}, dimensions={0} | all-to-all | bytes 66560 | tf_op jit(solution)/shard_map/all_to_all | solution.py:55
  308.4 7.9 %all_to_all.143 = f32[4,64,130]{2,1,0:T(8,128)S(1)} all-to-all(f32[4,64,130]{2,1,0:T(8,128)S(1)} %broadcast_in_dim.29), channel_id=1, replica_groups=mesh['hi_0'=4,'hi_1'=2,'lo_0'=8,'lo_1'=4] {'lo_1'}, dimensions={0} | all-to-all | bytes 266240 | tf_op jit(solution)/shard_map/all_to_all | solution.py:55
  319.0 10.5 %all_gather.20 = bf16[256,512]{1,0:T(8,128)(2,1)} all-gather(bf16[64,512]{1,0:T(8,128)(2,1)S(1)} %get-tuple-element.24), channel_id=1, replica_groups=mesh['hi_0'=4,'hi_1'=2,'lo_0'=8,'lo_1'=4] {'lo_1'}, dimensions={0}, use_global_device_ids=true | all-gather | bytes 327680 | tf_op jit(solution)/shard_map/all_gather | solution.py:16
  329.6 34.4 %all-gather.6.cloned.1.call-done = bf16[2048,512]{1,0:T(8,128)(2,1)} async-done(((bf16[256,512]{1,0:T(8,128)(2,1)}), bf16[2048,512]{1,0:T(8,128)(2,1)}) %all-gather.6.cloned.1.call-update) | async-done | bytes 2097168 | tf_op jit(solution)/shard_map/all_gather | solution.py:16
  364.0 2.8 fusion.229
  366.9 24.0 %all_to_all.144 = f32[8,64,512]{2,1,0:T(8,128)} all-to-all(f32[8,64,512]{2,1,0:T(8,128)S(1)} %bitcast.540), channel_id=1, replica_groups=mesh['hi_0'=4,'hi_1'=2,'lo_0'=8,'lo_1'=4] {'hi_0','hi_1'}, dimensions={0} | all-to-all | bytes 2097152 | tf_op jit(solution)/shard_map/all_to_all | solution.py:28
  393.6 18.7 %all_to_all.145 = f32[64,1,512]{2,1,0:T(1,128)S(1)} all-to-all(f32[64,1,512]{2,1,0:T(1,128)S(1)} %broadcast_in_dim.30), channel_id=1, replica_groups=mesh['hi_0'=4,'hi_1'=2,'lo_0'=8,'lo_1'=4] {'hi_1','lo_0','lo_1'}, dimensions={0} | all-to-all | bytes 262144 | tf_op jit(solution)/shard_map/all_to_all | solution.py:55
  412.4 6.7 %all_to_all.146 = f32[4,1,512]{2,1,0:T(1,128)S(1)} all-to-all(f32[4,1,512]{2,1,0:T(1,128)S(1)} %broadcast_in_dim.31), channel_id=1, replica_groups=mesh['hi_0'=4,'hi_1'=2,'lo_0'=8,'lo_1'=4] {'hi_0'}, dimensions={0} | all-to-all | bytes 16384 | tf_op jit(solution)/shard_map/all_to_all | solution.py:55
  423.6 1.4 fusion.10
  427.7 1.4 fusion.4
  430.5 1.4 fusion
  436.0 3.0 collective-permute-start.20
  439.0 2.3 collective-permute-start.21
  442.2 1.9 collective-permute-start.23
  449.0 1.5 multiply_reduce_fusion.1
  450.9 8.4 %all_to_all.147 = f32[4,64,130]{2,1,0:T(8,128)S(1)} all-to-all(f32[4,64,130]{2,1,0:T(8,128)S(1)} %copy.41), channel_id=1, replica_groups=mesh['hi_0'=4,'hi_1'=2,'lo_0'=8,'lo_1'=4] {'lo_1'}, dimensions={0} | all-to-all | bytes 266240 | tf_op jit(solution)/shard_map/all_to_all | solution.py:28
  459.4 19.1 %all_to_all.148 = f32[64,1,130]{2,1,0:T(1,128)S(1)} all-to-all(f32[64,1,130]{2,1,0:T(1,128)S(1)} %all_to_all.106), channel_id=1, replica_groups=mesh['hi_0'=4,'hi_1'=2,'lo_0'=8,'lo_1'=4] {'hi_0','hi_1','lo_0'}, dimensions={0} | all-to-all | bytes 66560 | tf_op jit(solution)/shard_map/all_to_all | solution.py:42
  478.6 13.7 %all_to_all.149 = f32[64,1,130]{2,1,0:T(1,128)S(1)} all-to-all(f32[64,1,130]{2,1,0:T(1,128)S(1)} %broadcast_in_dim.32), channel_id=1, replica_groups=mesh['hi_0'=4,'hi_1'=2,'lo_0'=8,'lo_1'=4] {'hi_0','hi_1','lo_0'}, dimensions={0} | all-to-all | bytes 66560 | tf_op jit(solution)/shard_map/all_to_all | solution.py:55
  492.4 7.9 %all_to_all.150 = f32[4,64,130]{2,1,0:T(8,128)S(1)} all-to-all(f32[4,64,130]{2,1,0:T(8,128)S(1)} %broadcast_in_dim.33), channel_id=1, replica_groups=mesh['hi_0'=4,'hi_1'=2,'lo_0'=8,'lo_1'=4] {'lo_1'}, dimensions={0} | all-to-all | bytes 266240 | tf_op jit(solution)/shard_map/all_to_all | solution.py:55
  503.9 10.5 %all_gather.22 = bf16[256,512]{1,0:T(8,128)(2,1)} all-gather(bf16[64,512]{1,0:T(8,128)(2,1)S(1)} %get-tuple-element.30), channel_id=1, replica_groups=mesh['hi_0'=4,'hi_1'=2,'lo_0'=8,'lo_1'=4] {'lo_1'}, dimensions={0}, use_global_device_ids=true | all-gather | bytes 327680 | tf_op jit(solution)/shard_map/all_gather | solution.py:16
  514.5 34.5 %all-gather.8.cloned.1.call-done = bf16[2048,512]{1,0:T(8,128)(2,1)} async-done(((bf16[256,512]{1,0:T(8,128)(2,1)}), bf16[2048,512]{1,0:T(8,128)(2,1)}) %all-gather.8.cloned.1.call-update) | async-done | bytes 2097168 | tf_op jit(solution)/shard_map/all_gather | solution.py:16
  548.9 2.8 fusion.230
  551.8 24.0 %all_to_all.151 = f32[8,64,512]{2,1,0:T(8,128)} all-to-all(f32[8,64,512]{2,1,0:T(8,128)S(1)} %bitcast.541), channel_id=1, replica_groups=mesh['hi_0'=4,'hi_1'=2,'lo_0'=8,'lo_1'=4] {'hi_0','hi_1'}, dimensions={0} | all-to-all | bytes 2097152 | tf_op jit(solution)/shard_map/all_to_all | solution.py:28
  578.5 18.7 %all_to_all.152 = f32[64,1,512]{2,1,0:T(1,128)S(1)} all-to-all(f32[64,1,512]{2,1,0:T(1,128)S(1)} %broadcast_in_dim.34), channel_id=1, replica_groups=mesh['hi_0'=4,'hi_1'=2,'lo_0'=8,'lo_1'=4] {'hi_1','lo_0','lo_1'}, dimensions={0} | all-to-all | bytes 262144 | tf_op jit(solution)/shard_map/all_to_all | solution.py:55
  597.3 6.5 %all_to_all.153 = f32[4,1,512]{2,1,0:T(1,128)S(1)} all-to-all(f32[4,1,512]{2,1,0:T(1,128)S(1)} %broadcast_in_dim.35), channel_id=1, replica_groups=mesh['hi_0'=4,'hi_1'=2,'lo_0'=8,'lo_1'=4] {'hi_0'}, dimensions={0} | all-to-all | bytes 16384 | tf_op jit(solution)/shard_map/all_to_all | solution.py:55
  604.6 2.1 multiply_subtract_fusion
  (329 shorter events, 100.1 us)
Async XLA Ops:
  7.2 171.7 %copy-start = (bf16[8,1,64,1,2048]{4,2,3,1,0:T(8,128)(2,1)S(1)}, bf16[8,1,64,1,2048]{4,2,3,1,0:T(8,128)(2,1)}, u32[]{:S(2)}) copy-start(bf16[8,1,64,1,2048]{4,2,3,1,0:T(8,128)(2,1)} %param.8) | copy-start | bytes 6291460
  7.2 171.7 %all-gather.4.cloned.1.call-start = ((), (), s32[]{:S(2)}) async-start(), calls=%async_computation.21 | async-start | bytes 2359296 | tf_op jit(solution)/shard_map/all_gather | solution.py:16
  12.9 60.7 %collective-permute-start.1 = (bf16[64,512]{1,0:T(8,128)(2,1)}, bf16[64,512]{1,0:T(8,128)(2,1)}, u32[]{:S(2)}, u32[]{:S(2)}) collective-permute-start(bf16[64,512]{1,0:T(8,128)(2,1)} %bitcast.505), channel_id=1, source_target_pairs={{0,2},{1,3},{2,0},{3,1},{4,6},{5,7},{6,4},{7,5},{8,10},{9,11},{10,... | collective-permute-start | bytes 196616 | tf_op jit(solution)/shard_map/ppermute | solution.py:35
  18.5 57.6 %collective-permute-start.2 = (bf16[64,512]{1,0:T(8,128)(2,1)}, bf16[64,512]{1,0:T(8,128)(2,1)}, u32[]{:S(2)}, u32[]{:S(2)}) collective-permute-start(bf16[64,512]{1,0:T(8,128)(2,1)} %bitcast.504), channel_id=1, source_target_pairs={{0,4},{1,5},{2,6},{3,7},{4,0},{5,1},{6,2},{7,3},{8,12},{9,13},{10,... | collective-permute-start | bytes 196616 | tf_op jit(solution)/shard_map/ppermute | solution.py:35
  22.1 57.9 %collective-permute-start.3 = (bf16[64,512]{1,0:T(8,128)(2,1)}, bf16[64,512]{1,0:T(8,128)(2,1)}, u32[]{:S(2)}, u32[]{:S(2)}) collective-permute-start(bf16[64,512]{1,0:T(8,128)(2,1)} %bitcast.503), channel_id=1, source_target_pairs={{0,8},{1,9},{2,10},{3,11},{4,12},{5,13},{6,14},{7,15},{8,0},{9,1},... | collective-permute-start | bytes 196616 | tf_op jit(solution)/shard_map/ppermute | solution.py:35
  25.1 14.1 %copy-start.1 = (f32[9,64,64]{2,1,0:T(8,128)S(1)}, f32[9,64,64]{2,1,0:T(8,128)}, u32[]{:S(2)}) copy-start(f32[9,64,64]{2,1,0:T(8,128)} %param.12) | copy-start | bytes 442372
  27.1 54.4 %collective-permute-start.4 = (bf16[64,512]{1,0:T(8,128)(2,1)}, bf16[64,512]{1,0:T(8,128)(2,1)}, u32[]{:S(2)}, u32[]{:S(2)}) collective-permute-start(bf16[64,512]{1,0:T(8,128)(2,1)} %bitcast.502), channel_id=1, source_target_pairs={{0,16},{1,17},{2,18},{3,19},{4,20},{5,21},{6,22},{7,23},{8,24},{9,... | collective-permute-start | bytes 196616 | tf_op jit(solution)/shard_map/ppermute | solution.py:35
  33.4 49.2 %collective-permute-start.5 = (bf16[64,512]{1,0:T(8,128)(2,1)}, bf16[64,512]{1,0:T(8,128)(2,1)}, u32[]{:S(2)}, u32[]{:S(2)}) collective-permute-start(bf16[64,512]{1,0:T(8,128)(2,1)} %bitcast.501), channel_id=1, source_target_pairs={{0,32},{32,0},{64,96},{96,64},{128,160},{160,128},{192,224},{224,1... | collective-permute-start | bytes 196616 | tf_op jit(solution)/shard_map/ppermute | solution.py:35
  45.6 33.2 %copy-start.13 = (f32[1,64,64]{2,0,1:T(1,128)}, f32[1,64,64]{2,0,1:T(1,128)S(1)}, u32[]{:S(2)}) copy-start(f32[1,64,64]{2,0,1:T(1,128)S(1)} %fusion.66) | copy-start | bytes 49156
  59.0 206.0 %copy-start.22 = (f32[512]{0:T(512)}, f32[512]{0:T(512)S(1)}, u32[]{:S(2)}) copy-start(f32[512]{0:T(512)S(1)} %mul.556) | copy-start | bytes 6148
  59.2 205.9 %copy-start.24 = (f32[512]{0:T(512)}, f32[512]{0:T(512)S(1)}, u32[]{:S(2)}) copy-start(f32[512]{0:T(512)S(1)} %mul.562) | copy-start | bytes 6148
  60.0 205.0 %copy-start.26 = (f32[512]{0:T(512)}, f32[512]{0:T(512)S(1)}, u32[]{:S(2)}) copy-start(f32[512]{0:T(512)S(1)} %mul.526) | copy-start | bytes 6148
  62.1 203.0 %copy-start.28 = (f32[512]{0:T(512)}, f32[512]{0:T(512)S(1)}, u32[]{:S(2)}) copy-start(f32[512]{0:T(512)S(1)} %mul.532) | copy-start | bytes 6148
  72.6 11.2 %copy-start.6 = (f32[1,64,64]{2,0,1:T(1,128)S(1)}, f32[1,64,64]{2,0,1:T(1,128)}, u32[]{:S(2)}) copy-start(f32[1,64,64]{2,0,1:T(1,128)} %fusion.58) | copy-start | bytes 49156
  73.6 10.2 %collective-permute-start.6 = (bf16[64,512]{1,0:T(8,128)(2,1)S(1)}, bf16[64,512]{1,0:T(8,128)(2,1)S(1)}, u32[]{:S(2)}, u32[]{:S(2)}) collective-permute-start(bf16[64,512]{1,0:T(8,128)(2,1)S(1)} %bitcast.587), channel_id=1, source_target_pairs={{0,64},{32,96},{64,0},{96,32},{128,192},{160,224},{192,128},{224,1... | collective-permute-start | bytes 196616 | tf_op jit(solution)/shard_map/ppermute | solution.py:35
  76.1 8.0 %collective-permute-start.7 = (bf16[64,512]{1,0:T(8,128)(2,1)S(1)}, bf16[64,512]{1,0:T(8,128)(2,1)S(1)}, u32[]{:S(2)}, u32[]{:S(2)}) collective-permute-start(bf16[64,512]{1,0:T(8,128)(2,1)S(1)} %bitcast.582), channel_id=1, source_target_pairs={{0,128},{32,160},{64,192},{96,224},{128,0},{160,32},{192,64},{224,... | collective-permute-start | bytes 196616 | tf_op jit(solution)/shard_map/ppermute | solution.py:35
  80.0 4.4 collective-permute-start
  133.6 103.0 %copy-start.46 = (f32[512]{0:T(512)}, f32[512]{0:T(512)S(1)}, u32[]{:S(2)}) copy-start(f32[512]{0:T(512)S(1)} %get-tuple-element.18) | copy-start | bytes 6148
  182.7 9.3 %copy-start.54 = (f32[2]{0:T(128)S(1)}, f32[2]{0:T(128)}, u32[]{:S(2)}) copy-start(f32[2]{0:T(128)} %param.14) | copy-start | bytes 28
  182.7 24.4 %all-to-all-start.4 = ((f32[8,64,512]{2,1,0:T(8,128)}), f32[8,64,512]{2,1,0:T(8,128)}, u32[]{:S(2)}, u32[]{:S(2)}) async-start(f32[8,64,512]{2,1,0:T(8,128)} %bitcast.539), calls=%async_computation.4 | async-start | bytes 2097152 | tf_op jit(solution)/shard_map/all_to_all | solution.py:28
  192.6 44.0 %copy-start.48 = (s32[512]{0:T(512)S(1)}, s32[512]{0:T(512)}, u32[]{:S(2)}) copy-start(s32[512]{0:T(512)} %param.15) | copy-start | bytes 6148
  229.1 7.4 %all-to-all-start.6 = ((f32[4,1,512]{2,1,0:T(1,128)}), f32[4,1,512]{2,1,0:T(1,128)S(1)}, u32[]{:S(2)}, u32[]{:S(2)}) async-start(f32[4,1,512]{2,1,0:T(1,128)} %broadcast_in_dim.27), calls=%async_computation.6 | async-start | bytes 16384 | tf_op jit(solution)/shard_map/all_to_all | solution.py:55
  232.4 131.6 %all-gather.6.cloned.1.call-start = ((), (), s32[]{:S(2)}) async-start(), calls=%async_computation.22 | async-start | bytes 2359296 | tf_op jit(solution)/shard_map/all_gather | solution.py:16
  232.7 7.7 %copy-start.18 = (f32[33280]{0:T(1024)}, f32[33280]{0:T(1024)S(1)}, u32[]{:S(2)}) copy-start(f32[33280]{0:T(1024)S(1)} %reshape_reshape.19) | copy-start | bytes 399364
  250.0 8.7 %copy-start.16 = (f32[1,64,64]{2,0,1:T(1,128)S(1)}, f32[1,64,64]{2,0,1:T(1,128)}, u32[]{:S(2)}) copy-start(f32[1,64,64]{2,0,1:T(1,128)} %fusion.68) | copy-start | bytes 49156
  250.1 10.9 %copy-start.14 = (f32[1,64,64]{2,0,1:T(1,128)S(1)}, f32[1,64,64]{2,0,1:T(1,128)}, u32[]{:S(2)}) copy-start(f32[1,64,64]{2,0,1:T(1,128)} %copy-done.13) | copy-start | bytes 49156
  250.1 8.3 %collective-permute-start.9 = (bf16[64,512]{1,0:T(8,128)(2,1)S(1)}, bf16[64,512]{1,0:T(8,128)(2,1)S(1)}, u32[]{:S(2)}, u32[]{:S(2)}) collective-permute-start(bf16[64,512]{1,0:T(8,128)(2,1)S(1)} %bitcast.595), channel_id=1, source_target_pairs={{0,2},{1,3},{2,0},{3,1},{4,6},{5,7},{6,4},{7,5},{8,10},{9,11},{10,... | collective-permute-start | bytes 196616 | tf_op jit(solution)/shard_map/ppermute | solution.py:35
  251.4 10.4 %copy-start.11 = (f32[1,64,64]{2,0,1:T(1,128)S(1)}, f32[1,64,64]{2,0,1:T(1,128)}, u32[]{:S(2)}) copy-start(f32[1,64,64]{2,0,1:T(1,128)} %fusion.64) | copy-start | bytes 49156
  251.4 7.6 %collective-permute-start.10 = (bf16[64,512]{1,0:T(8,128)(2,1)S(1)}, bf16[64,512]{1,0:T(8,128)(2,1)S(1)}, u32[]{:S(2)}, u32[]{:S(2)}) collective-permute-start(bf16[64,512]{1,0:T(8,128)(2,1)S(1)} %bitcast.594), channel_id=1, source_target_pairs={{0,4},{1,5},{2,6},{3,7},{4,0},{5,1},{6,2},{7,3},{8,12},{9,13},{10,... | collective-permute-start | bytes 196616 | tf_op jit(solution)/shard_map/ppermute | solution.py:35
  252.3 9.0 %collective-permute-start.11 = (bf16[64,512]{1,0:T(8,128)(2,1)S(1)}, bf16[64,512]{1,0:T(8,128)(2,1)S(1)}, u32[]{:S(2)}, u32[]{:S(2)}) collective-permute-start(bf16[64,512]{1,0:T(8,128)(2,1)S(1)} %bitcast.592), channel_id=1, source_target_pairs={{0,8},{1,9},{2,10},{3,11},{4,12},{5,13},{6,14},{7,15},{8,0},{9,1},... | collective-permute-start | bytes 196616 | tf_op jit(solution)/shard_map/ppermute | solution.py:35
  252.9 9.2 %copy-start.9 = (f32[1,64,64]{2,0,1:T(1,128)S(1)}, f32[1,64,64]{2,0,1:T(1,128)}, u32[]{:S(2)}) copy-start(f32[1,64,64]{2,0,1:T(1,128)} %fusion.62) | copy-start | bytes 49156
  252.9 9.1 %collective-permute-start.12 = (bf16[64,512]{1,0:T(8,128)(2,1)S(1)}, bf16[64,512]{1,0:T(8,128)(2,1)S(1)}, u32[]{:S(2)}, u32[]{:S(2)}) collective-permute-start(bf16[64,512]{1,0:T(8,128)(2,1)S(1)} %bitcast.590), channel_id=1, source_target_pairs={{0,16},{1,17},{2,18},{3,19},{4,20},{5,21},{6,22},{7,23},{8,24},{9,... | collective-permute-start | bytes 196616 | tf_op jit(solution)/shard_map/ppermute | solution.py:35
  256.0 6.4 %collective-permute-start.13 = (bf16[64,512]{1,0:T(8,128)(2,1)S(1)}, bf16[64,512]{1,0:T(8,128)(2,1)S(1)}, u32[]{:S(2)}, u32[]{:S(2)}) collective-permute-start(bf16[64,512]{1,0:T(8,128)(2,1)S(1)} %bitcast.588), channel_id=1, source_target_pairs={{0,32},{32,0},{64,96},{96,64},{128,160},{160,128},{192,224},{224,1... | collective-permute-start | bytes 196616 | tf_op jit(solution)/shard_map/ppermute | solution.py:35
  258.4 4.3 collective-permute-start.14
  259.1 4.7 collective-permute-start.15
  261.3 3.5 collective-permute-start.8
  308.4 9.7 %copy-start.47 = (f32[512]{0:T(512)S(1)}, f32[512]{0:T(512)}, u32[]{:S(2)}) copy-start(f32[512]{0:T(512)} %copy-done.46) | copy-start | bytes 6148
  329.5 219.4 %all-gather.8.cloned.1.call-start = ((), (), s32[]{:S(2)}) async-start(), calls=%async_computation.23 | async-start | bytes 2359296 | tf_op jit(solution)/shard_map/all_gather | solution.py:16
  390.9 28.3 %copy-start.20 = (f32[512]{0:T(512)S(1)}, f32[512]{0:T(512)}, u32[]{:S(2)}) copy-start(f32[512]{0:T(512)} %copy-done.19) | copy-start | bytes 6148
  390.9 28.3 %copy-start.49 = (s32[512]{0:T(512)S(1)}, s32[512]{0:T(512)}, u32[]{:S(2)}) copy-start(s32[512]{0:T(512)} %param.15) | copy-start | bytes 6148
  433.3 8.6 %copy-start.17 = (f32[1,64,64]{2,0,1:T(1,128)S(1)}, f32[1,64,64]{2,0,1:T(1,128)}, u32[]{:S(2)}) copy-start(f32[1,64,64]{2,0,1:T(1,128)} %fusion.68) | copy-start | bytes 49156
  433.3 10.8 %copy-start.15 = (f32[1,64,64]{2,0,1:T(1,128)S(1)}, f32[1,64,64]{2,0,1:T(1,128)}, u32[]{:S(2)}) copy-start(f32[1,64,64]{2,0,1:T(1,128)} %copy-done.13) | copy-start | bytes 49156
  433.3 8.1 %collective-permute-start.17 = (bf16[64,512]{1,0:T(8,128)(2,1)S(1)}, bf16[64,512]{1,0:T(8,128)(2,1)S(1)}, u32[]{:S(2)}, u32[]{:S(2)}) collective-permute-start(bf16[64,512]{1,0:T(8,128)(2,1)S(1)} %bitcast.596), channel_id=1, source_target_pairs={{0,2},{1,3},{2,0},{3,1},{4,6},{5,7},{6,4},{7,5},{8,10},{9,11},{10,... | collective-permute-start | bytes 196616 | tf_op jit(solution)/shard_map/ppermute | solution.py:35
  434.7 10.5 %copy-start.12 = (f32[1,64,64]{2,0,1:T(1,128)S(1)}, f32[1,64,64]{2,0,1:T(1,128)}, u32[]{:S(2)}) copy-start(f32[1,64,64]{2,0,1:T(1,128)} %fusion.64) | copy-start | bytes 49156
  434.7 7.5 %collective-permute-start.18 = (bf16[64,512]{1,0:T(8,128)(2,1)S(1)}, bf16[64,512]{1,0:T(8,128)(2,1)S(1)}, u32[]{:S(2)}, u32[]{:S(2)}) collective-permute-start(bf16[64,512]{1,0:T(8,128)(2,1)S(1)} %bitcast.593), channel_id=1, source_target_pairs={{0,4},{1,5},{2,6},{3,7},{4,0},{5,1},{6,2},{7,3},{8,12},{9,13},{10,... | collective-permute-start | bytes 196616 | tf_op jit(solution)/shard_map/ppermute | solution.py:35
  435.6 8.8 %collective-permute-start.19 = (bf16[64,512]{1,0:T(8,128)(2,1)S(1)}, bf16[64,512]{1,0:T(8,128)(2,1)S(1)}, u32[]{:S(2)}, u32[]{:S(2)}) collective-permute-start(bf16[64,512]{1,0:T(8,128)(2,1)S(1)} %bitcast.591), channel_id=1, source_target_pairs={{0,8},{1,9},{2,10},{3,11},{4,12},{5,13},{6,14},{7,15},{8,0},{9,1},... | collective-permute-start | bytes 196616 | tf_op jit(solution)/shard_map/ppermute | solution.py:35
  436.0 9.5 %copy-start.10 = (f32[1,64,64]{2,0,1:T(1,128)S(1)}, f32[1,64,64]{2,0,1:T(1,128)}, u32[]{:S(2)}) copy-start(f32[1,64,64]{2,0,1:T(1,128)} %fusion.62) | copy-start | bytes 49156
  436.0 9.4 %collective-permute-start.20 = (bf16[64,512]{1,0:T(8,128)(2,1)S(1)}, bf16[64,512]{1,0:T(8,128)(2,1)S(1)}, u32[]{:S(2)}, u32[]{:S(2)}) collective-permute-start(bf16[64,512]{1,0:T(8,128)(2,1)S(1)} %bitcast.586), channel_id=1, source_target_pairs={{0,16},{1,17},{2,18},{3,19},{4,20},{5,21},{6,22},{7,23},{8,24},{9,... | collective-permute-start | bytes 196616 | tf_op jit(solution)/shard_map/ppermute | solution.py:35
  439.0 6.7 %collective-permute-start.21 = (bf16[64,512]{1,0:T(8,128)(2,1)S(1)}, bf16[64,512]{1,0:T(8,128)(2,1)S(1)}, u32[]{:S(2)}, u32[]{:S(2)}) collective-permute-start(bf16[64,512]{1,0:T(8,128)(2,1)S(1)} %bitcast.585), channel_id=1, source_target_pairs={{0,32},{32,0},{64,96},{96,64},{128,160},{160,128},{192,224},{224,1... | collective-permute-start | bytes 196616 | tf_op jit(solution)/shard_map/ppermute | solution.py:35
  441.5 4.6 collective-permute-start.22
  442.2 6.1 copy-start.23
  442.2 6.1 copy-start.25
  442.2 6.1 copy-start.27
  442.2 6.1 copy-start.29
  442.2 6.1 copy-start.32
  442.2 6.1 copy-start.35
  442.2 6.1 copy-start.38
  442.2 6.1 copy-start.41
  442.2 4.7 collective-permute-start.23
  444.4 3.6 collective-permute-start.16
  492.4 9.7 %copy-start.21 = (f32[512]{0:T(512)S(1)}, f32[512]{0:T(512)}, u32[]{:S(2)}) copy-start(f32[512]{0:T(512)} %copy-done.19) | copy-start | bytes 6148
  575.8 28.1 %copy-start.50 = (s32[512]{0:T(512)S(1)}, s32[512]{0:T(512)}, u32[]{:S(2)}) copy-start(s32[512]{0:T(512)} %param.15) | copy-start | bytes 6148
  575.8 28.8 %copy-start.43 = (f32[512]{0:T(512)S(1)}, f32[512]{0:T(512)}, u32[]{:S(2)}) copy-start(f32[512]{0:T(512)} %copy-done.42) | copy-start | bytes 6148
  575.8 28.8 %copy-start.45 = (f32[512]{0:T(512)S(1)}, f32[512]{0:T(512)}, u32[]{:S(2)}) copy-start(f32[512]{0:T(512)} %copy-done.44) | copy-start | bytes 6148
  (20 other events, 80.2 us)
Sparse Core Ops, SparseCore 0:
  144.5 34.3 all-gather.3
  329.7 34.3 all-gather.5
  514.6 34.2 all-gather.7
where the time goes:
time: 622 us; the launch traced here: 614 us
  blocking collectives  293 us (47%)
  waiting for transfers between devices  125 us (20%)
  matrix products  73.4 us (12%)
  starting transfers between devices  53.4 us (9%)
  local copies, waits for them, and re-layouts  27.3 us (4%)
  other arithmetic  26.7 us (4%)
  between operations  15.7 us (3%)
    all_to_all x11, blocking collectives, from_everyone(): return lax.all_to_all(copies, axis, split_axis=0, concat_axis=0, tiled=True)  135 us
    all_gather x3, waiting for transfers between devices, gather_axes(): nearer = lax.all_gather(array, axes[-1], axis=dim, tiled=True)  103 us
    all_to_all x5, blocking collectives, sent_and_summed(): lax.all_to_all(tiles, axis, split_axis=0, concat_axis=0, tiled=True)  73 us
    all_to_all x3, blocking collectives, sum_by_axis(): lax.all_to_all(nearer, far, split_axis=0, concat_axis=0, tiled=True)  53.4 us
    ppermute x24, starting transfers between devices, from_partner(): return lax.ppermute(value, axis, pairs)  40.7 us
    dot_general x24, matrix products, level_pieces(): own_part = jnp.einsum('l,lrb->rb', select, coefficients)  32.9 us
    all_gather x3, blocking collectives, gather_axes(): nearer = lax.all_gather(array, axes[-1], axis=dim, tiled=True)  31.5 us
    all_to_all x1, waiting for transfers between devices, sent_and_summed(): lax.all_to_all(tiles, axis, split_axis=0, concat_axis=0, tiled=True)  14.5 us
  transfers between devices with their start and end apart: 29, of which 9 were waited for; matrix products, arithmetic and copies ran while one was open for 9% of the time, Pallas kernels for 0%

commit v1 on v0

v1 whole, which is shorter than its diff:
```python
import functools

import jax
import jax.numpy as jnp
from jax import lax
from jax.experimental import pallas as pl
from jax.experimental.pallas import tpu as pltpu
from jax.sharding import Mesh
from jax.sharding import PartitionSpec as P

ITERS = 3
LO = ("z", "x")
HI = ("y", "c")
HI_LO = ("y", "c", "z", "x")
NY, NC, NZ, NX = 4, 2, 8, 4
HIGHEST = lax.Precision.HIGHEST
F32, BF16 = jnp.float32, jnp.bfloat16

GATHER_KEYS = (
    [("az", k, 0) for k in (7, 1, 6, 2, 5, 3)]
    + [("az+", 4, 0), ("az-", 4, 0)]
    + [(kind, k, 0) for kind in ("ax+", "ax-", "af+", "af-") for k in range(8)]
    + [(kind, 0, 0) for kind in ("bx+", "bx-", "bf+", "bf-")]
    + [("bz", k, d) for k in (7, 1, 6, 2, 5, 3) for d in range(4)]
    + [(kind, 4, d) for kind in ("bz+", "bz-") for d in range(4)]
)
GATHER_ID = {key: n for n, key in enumerate(GATHER_KEYS)}
ROWS = {
    "az": (0, 32), "az+": (0, 16), "az-": (16, 16),
    "ax+": (0, 32), "ax-": (0, 32), "af+": (0, 16), "af-": (16, 16),
    "bx+": (32, 32), "bx-": (32, 32), "bf+": (32, 16), "bf-": (48, 16),
    "bz": (32, 32), "bz+": (32, 16), "bz-": (48, 16),
}


def dot(a, b, precision=HIGHEST):
    return jnp.dot(a, b, precision=precision, preferred_element_type=F32)


def kernel(
    var_ref, grm_ref, rhs_ref, diag_ref, bt_ref, bk_ref, bc_ref, kc_ref, iters_ref,
    x_ref, r_ref,
    g_ref, v_ref, vc_ref, co_ref, cb_ref, xb_ref,
    y_ref, u_ref, w_ref, p_ref, s_ref, q_ref, ul_ref, ml_ref, tu_ref, tq_ref,
    p1_ref, r1_ref, q2_ref, qb_ref, r2_ref,
    pc_ref, rc_ref, ack_ref, bck_ref,
    as_ref, ah_ref, bs_ref, bx_ref, zs_ref, bz_ref, xa_ref, ta_ref,
    row_ref,
    g_sem, ex_send, ex_recv, ag_send, ag_recv, r1_send, r1_recv, r2_send, r2_recv,
    ar_send, ar_recv, mc_send, mc_recv,
):
    y, c, z, x = (lax.axis_index(name) for name in HI_LO)
    hi = y * 2 + c

    def dev(**where):
        return where

    def hi_dev(d):
        to = (hi + d) % 8
        return {"y": to // 2, "c": to % 2}

    def remote(src, dst, send, recv, to):
        return pltpu.make_async_remote_copy(
            src_ref=src, dst_ref=dst, send_sem=send, recv_sem=recv,
            device_id=to, device_id_type=pl.DeviceIdType.MESH,
        )

    loads = []
    for k in range(NZ):
        at = pl.multiple_of((z + k) % NZ * 256, 256)
        loads.append(
            pltpu.make_async_copy(
                grm_ref.at[:, :, pl.ds(at, 256)], g_ref.at[:, :, pl.ds(k * 256, 256)], g_sem.at[k]
            )
        )
        loads[-1].start()

    barrier = pltpu.get_barrier_semaphore()
    near = [{"x": (x + d) % NX} for d in range(1, NX)]
    near += [{"z": (z + d) % NZ} for d in range(1, NZ)]
    near += [hi_dev(d) for d in range(1, 8)]
    for to in near:
        pl.semaphore_signal(barrier, inc=1, device_id=to, device_id_type=pl.DeviceIdType.MESH)
    zero = jnp.zeros((64, 512), F32)
    for ref in (u_ref, w_ref, p_ref, s_ref, q_ref, tq_ref, x_ref):
        ref[...] = zero
    r_ref[...] = rhs_ref[...]
    y_ref[...] = rhs_ref[...]
    row_ref[...] = jnp.ones_like(row_ref)
    vc_ref[0, x] = bc_ref[...]
    bck_ref[...] = dot(bc_ref[:, :64].astype(F32) + bc_ref[:, 64:].astype(F32), kc_ref[...])
    pl.semaphore_wait(barrier, len(near))

    def coarse_z(d):
        return remote(vc_ref.at[0, x], vc_ref.at[8 - d, x], mc_send.at[0], mc_recv.at[d - 1], {"z": (z + d) % NZ})

    def coarse_x(d):
        return remote(vc_ref.at[:, x], vc_ref.at[:, x], mc_send.at[1], mc_recv.at[6 + d], {"x": (x + d) % NX})

    def coarse_x_in(d):
        at = vc_ref.at[:, (x + NX - d) % NX]
        return remote(at, at, mc_send.at[1], mc_recv.at[6 + d], {"x": (x + d) % NX})

    def coarse_r(d):
        return remote(pc_ref.at[(hi + d) % 8], rc_ref.at[d - 1], mc_send.at[2], mc_recv.at[9 + d], hi_dev(d))

    for d in range(1, NZ):
        coarse_z(d).start()

    partners = [
        {"x": x + 1 - 2 * (x % 2)}, {"x": (x + 2) % 4},
        {"z": z + 1 - 2 * (z % 2)}, {"z": z + 2 - 4 * ((z // 2) % 2)}, {"z": (z + 4) % 8},
        {"c": 1 - c}, {"y": y + 1 - 2 * (y % 2)}, {"y": (y + 2) % 4},
    ]

    def exchange(i, g):
        return remote(cb_ref.at[i, g], xb_ref.at[i, g], ex_send.at[i], ex_recv.at[i, g], partners[g])

    def piece(i, kind, k, d, slot_from, slot_to, to):
        at, rows = ROWS[kind]
        return remote(
            v_ref.at[i, slot_from, pl.ds(at, rows)], v_ref.at[i, slot_to, pl.ds(at, rows)],
            ag_send.at[i], ag_recv.at[i, GATHER_ID[kind, k, d]], to,
        )

    def slot(k, d):
        return k * NX + (x + d) % NX

    up, down = {"z": (z + 1) % NZ}, {"z": (z + NZ - 1) % NZ}
    right, left = {"x": (x + 1) % NX}, {"x": (x + NX - 1) % NX}

    def along_z(i, kind, k, d):
        if k in (0, 7, 6, 5):
            to = (k - 1) % 8
            name = kind + "+" if to == 4 else kind
            piece(i, name, to, d, slot(k, d), slot(to, d), up).start()
        if k in (0, 1, 2, 3):
            to = k + 1
            name = kind + "-" if to == 4 else kind
            piece(i, name, to, d, slot(k, d), slot(to, d), down).start()

    def got(i, kind, k, d, where):
        piece(i, kind, k, d, where, where, up).wait_recv()

    def along_x(i, kind, k):
        piece(i, kind + "+", k, 0, slot(k, 0), slot(k, 0), right).start()
        piece(i, kind + "-", k, 0, slot(k, 0), slot(k, 0), left).start()

    def turn_x(i, kind, name, k):
        got(i, kind + "+", k, 0, slot(k, 3))
        piece(i, name + "+", k, 0, slot(k, 3), slot(k, 3), right).start()
        got(i, kind + "-", k, 0, slot(k, 1))
        piece(i, name + "-", k, 0, slot(k, 1), slot(k, 1), left).start()

    def far_x(i, name, k):
        got(i, name + "+", k, 0, slot(k, 2))
        got(i, name + "-", k, 0, slot(k, 2))

    def came_z(i, kind, k, d):
        if k == 4:
            got(i, kind + "+", 4, d, slot(4, d))
            got(i, kind + "-", 4, d, slot(4, d))
        else:
            got(i, kind, k, d, slot(k, d))
            along_z(i, kind, k, d)

    def gather_start(i):
        along_z(i, "az", 0, 0)
        along_x(i, "bx", 0)
        along_x(i, "ax", 0)
        along_z(i, "bz", 0, 0)

    def gather_1(i):
        for k in (7, 1):
            came_z(i, "az", k, 0)
            along_x(i, "ax", k)
        turn_x(i, "bx", "bf", 0)
        along_z(i, "bz", 0, 3)
        along_z(i, "bz", 0, 1)
        turn_x(i, "ax", "af", 0)
        for k in (7, 1):
            came_z(i, "bz", k, 0)

    def gather_2(i):
        for k in (6, 2):
            came_z(i, "az", k, 0)
            along_x(i, "ax", k)
        far_x(i, "bf", 0)
        along_z(i, "bz", 0, 2)
        for k in (7, 1):
            turn_x(i, "ax", "af", k)
        for d in (3, 1):
            for k in (7, 1):
                came_z(i, "bz", k, d)
        for k in (6, 2):
            came_z(i, "bz", k, 0)

    def gather_3(i):
        for k in (5, 3):
            came_z(i, "az", k, 0)
            along_x(i, "ax", k)
        for k in (6, 2):
            turn_x(i, "ax", "af", k)
        for k in (7, 1):
            came_z(i, "bz", k, 2)
        for d in (3, 1):
            for k in (6, 2):
                came_z(i, "bz", k, d)
        for k in (5, 3):
            came_z(i, "bz", k, 0)

    def gather_4(i):
        came_z(i, "az", 4, 0)
        along_x(i, "ax", 4)
        for k in (5, 3):
            turn_x(i, "ax", "af", k)
        for k in (6, 2):
            came_z(i, "bz", k, 2)
        for d in (3, 1):
            for k in (5, 3):
                came_z(i, "bz", k, d)
        came_z(i, "bz", 4, 0)

    def gather_5(i):
        turn_x(i, "ax", "af", 4)
        for k in (5, 3):
            came_z(i, "bz", k, 2)
        for d in (3, 1, 2):
            came_z(i, "bz", 4, d)
        for k in range(8):
            far_x(i, "af", k)

    def sum_hi(j, d):
        return remote(as_ref.at[j, (hi + d) % 8], ah_ref.at[j, d - 1], ar_send.at[j, 0], ar_recv.at[j, d - 1], hi_dev(d))

    def sum_x(j, d):
        return remote(bs_ref.at[j, (x + d) % 4], bx_ref.at[j, d - 1], ar_send.at[j, 1], ar_recv.at[j, 6 + d], {"x": (x + d) % NX})

    def sum_z(j, d):
        return remote(zs_ref.at[j], bz_ref.at[j, d - 1], ar_send.at[j, 2], ar_recv.at[j, 9 + d], {"z": (z + d) % NZ})

    def all_x(j, d):
        return remote(xa_ref.at[j, x], xa_ref.at[j, x], ar_send.at[j, 3], ar_recv.at[j, 16 + d], {"x": (x + d) % NX})

    def all_x_in(j, d):
        at = xa_ref.at[j, (x + NX - d) % NX]
        return remote(at, at, ar_send.at[j, 3], ar_recv.at[j, 16 + d], {"x": (x + d) % NX})

    def all_hi(j, d):
        return remote(ta_ref.at[j, hi], ta_ref.at[j, hi], ar_send.at[j, 4], ar_recv.at[j, 19 + d], hi_dev(d))

    def all_hi_in(j, d):
        at = ta_ref.at[j, (hi + 8 - d) % 8]
        return remote(at, at, ar_send.at[j, 4], ar_recv.at[j, 19 + d], hi_dev(d))

    def sums_start(j, total):
        gamma = jnp.sum(r_ref[...] * u_ref[...], axis=0, keepdims=True)
        delta = jnp.sum(u_ref[...] * w_ref[...], axis=0, keepdims=True)
        eta = jnp.sum(u_ref[...] * s_ref[...] + p_ref[...] * w_ref[...], axis=0, keepdims=True)
        line = lax.broadcasted_iota(jnp.int32, (8, 512), 0)
        rows = jnp.where(line == 0, gamma, jnp.where(line == 1, delta, jnp.where(line == 2, eta, 0.0)))
        for h in range(8):
            as_ref[j, h, 0:8, :] = total[h * 8 : (h + 1) * 8] if total is not None else jnp.zeros((8, 512), F32)
            as_ref[j, h, 8:16, :] = rows
        for d in range(1, 8):
            sum_hi(j, d).start()

    def sums_1(j):
        whole = as_ref[j, hi]
        for d in range(1, 8):
            sum_hi(j, d).wait_recv()
            whole = whole + ah_ref[j, d - 1]
        for k in range(4):
            bs_ref[j, k] = whole[:, k * 128 : (k + 1) * 128]
        for d in range(1, 4):
            sum_x(j, d).start()

    def sums_2(j):
        whole = bs_ref[j, x]
        for d in range(1, 4):
            sum_x(j, d).wait_recv()
            whole = whole + bx_ref[j, d - 1]
        zs_ref[j] = whole
        for d in range(1, 8):
            sum_z(j, d).start()

    def sums_3(j):
        whole = zs_ref[j]
        for d in range(1, 8):
            sum_z(j, d).wait_recv()
            whole = whole + bz_ref[j, d - 1]
        xa_ref[j, x] = whole
        for d in range(1, 4):
            all_x(j, d).start()

    def sums_4(j, coarse):
        for d in range(1, 4):
            all_x_in(j, d).wait_recv()
        if coarse:
            for k in range(4):
                ta_ref[j, hi, k] = xa_ref[j, k, 0:8, :]
            for d in range(1, 8):
                all_hi(j, d).start()

    def sums_of(j):
        return [
            jnp.concatenate([xa_ref[j, k, 8 + n : 9 + n, :] for k in range(4)], axis=1) for n in range(3)
        ]

    def sums_5(j):
        for d in range(1, 8):
            all_hi_in(j, d).wait_recv()
        return jnp.concatenate([ta_ref[j, :, k].reshape(64, 128) for k in range(4)], axis=1)

    def to_core(i):
        return remote(p1_ref.at[i], r1_ref.at[i], r1_send.at[i], r1_recv.at[i], {"c": 1 - c})

    def to_y(i, d):
        return remote(qb_ref.at[i, d - 1], r2_ref.at[i, d - 1], r2_send.at[i], r2_recv.at[i, d - 1], {"y": (y + d) % NY})

    def rows_of(core):
        return jnp.concatenate([g_ref[2 * k + core] for k in range(4)], axis=0)

    def times_grm(i):
        dense = v_ref[i].reshape(2048, 512)
        p1_ref[i] = dot(rows_of(1 - c), dense, None).astype(BF16).reshape(4, 64, 512)
        to_core(i).start()
        own = dot(rows_of(c), dense, None).reshape(4, 64, 512)
        to_core(i).wait_recv()
        q2_ref[...] = own + r1_ref[i].astype(F32)
        for d in range(1, 4):
            qb_ref[i, d - 1] = q2_ref[(y + d) % NY].astype(BF16)
            to_y(i, d).start()

    def product(i):
        for d in range(1, 4):
            to_y(i, d).wait_recv()
        whole = q2_ref[y]
        for d in range(1, 4):
            whole = whole + r2_ref[i, d - 1].astype(F32)
        return whole

    def weights(step, gamma, delta, eta):
        beta = jnp.where(step == 0, 0.0, gamma / row_ref[0:1])
        curve = delta + beta * eta + beta * beta * row_ref[1:2]
        alpha = gamma / curve
        row_ref[0:1] = gamma
        row_ref[1:2] = curve
        row_ref[2:3] = beta
        row_ref[3:4] = alpha
        return beta, alpha, jnp.where(step < iters_ref[...], alpha, 0.0)

    def body(i, carry):
        coeff = dot(bt_ref[...], y_ref[...])
        co_ref[...] = coeff[:512]
        cb_ref[i] = coeff[:512].astype(BF16).reshape(8, 64, 512)
        sums_start(i, coeff[512:])
        for g in (4, 3, 1, 7, 2, 0, 6, 5):
            exchange(i, g).start()

        @pl.when(i == 0)
        def _():
            for d in range(1, NZ):
                coarse_z(d).wait_recv()
            for d in range(1, NX):
                coarse_x(d).start()

        sums_1(i)
        sums_2(i)
        for g in (5, 6, 0, 2, 7, 1, 3, 4):
            exchange(i, g).wait_recv()
        both = co_ref[...] + xb_ref[i].astype(F32).reshape(512, 512)
        ml_ref[...] = diag_ref[:, 0:1] * y_ref[...] + dot(bk_ref[...], both)
        sums_3(i)
        sums_4(i, True)

        @pl.when(i == 0)
        def _():
            ul_ref[...] = ml_ref[...]

        @pl.when(i > 0)
        def _():
            beta, alpha, stepsize = weights(i - 1, *sums_of(i))
            q = ml_ref[...] + beta * q_ref[...]
            ul_ref[...] = ul_ref[...] - alpha * q
            q_ref[...] = q

        v_ref[i, x] = ul_ref[...].astype(BF16)
        gather_start(i)

        @pl.when(i > 0)
        def _():
            beta = row_ref[2:3]
            stepsize = jnp.where(i - 1 < iters_ref[...], row_ref[3:4], 0.0)
            p = u_ref[...] + beta * p_ref[...]
            s = w_ref[...] + beta * s_ref[...]
            x_ref[...] = x_ref[...] + stepsize * p
            r_ref[...] = r_ref[...] - stepsize * s
            p_ref[...] = p
            s_ref[...] = s

        gather_1(i)
        gather_2(i)
        gather_3(i)

        @pl.when(i == 0)
        def _():
            for d in range(1, NX):
                coarse_x_in(d).wait_recv()
            for load in loads:
                load.wait()
            part = dot(g_ref[...].reshape(512, 2048), vc_ref[...].reshape(2048, 128), None)
            pc_ref[...] = part.reshape(8, 64, 128)
            for d in range(1, 8):
                coarse_r(d).start()

        gather_4(i)
        gather_5(i)
        times_grm(i)
        coarse = sums_5(i)

        @pl.when(i == 0)
        def _():
            whole = pc_ref[hi]
            for d in range(1, 8):
                coarse_r(d).wait_recv()
                whole = whole + rc_ref[d - 1]
            own = bc_ref[:, :64].astype(F32) + bc_ref[:, 64:].astype(F32)
            ac = var_ref[0] * (whole[:, :64] + whole[:, 64:]) + var_ref[1] * own
            ack_ref[...] = dot(ac, kc_ref[...])
            tu_ref[...] = coarse

        @pl.when(i > 0)
        def _():
            tq = coarse + row_ref[2:3] * tq_ref[...]
            tu_ref[...] = tu_ref[...] - row_ref[3:4] * tq
            tq_ref[...] = tq

        u_ref[...] = ul_ref[...] + dot(bck_ref[...], tu_ref[...])
        shift = var_ref[1] * ul_ref[...] + dot(ack_ref[...], tu_ref[...])
        w = var_ref[0] * product(i) + shift
        w_ref[...] = w
        y_ref[...] = w
        return carry

    lax.fori_loop(0, ITERS, body, 0)
    sums_start(ITERS, None)
    sums_1(ITERS)
    sums_2(ITERS)
    sums_3(ITERS)
    sums_4(ITERS, False)
    beta, alpha, stepsize = weights(ITERS - 1, *sums_of(ITERS))
    x_ref[...] = x_ref[...] + stepsize * (u_ref[...] + beta * p_ref[...])
    r_ref[...] = r_ref[...] - stepsize * (w_ref[...] + beta * s_ref[...])

    def left_all(ref, sem):
        pltpu.make_async_copy(ref, ref, sem).wait()

    for i in range(ITERS):
        left_all(cb_ref.at[i], ex_send.at[i])
        left_all(v_ref.at[i, pl.ds(0, 31)], ag_send.at[i])
        left_all(p1_ref.at[i], r1_send.at[i])
        left_all(qb_ref.at[i], r2_send.at[i])
    for j in range(ITERS + 1):
        left_all(ah_ref.at[j], ar_send.at[j, 0])
        left_all(bx_ref.at[j], ar_send.at[j, 1])
        left_all(bz_ref.at[j], ar_send.at[j, 2])
        left_all(bx_ref.at[j], ar_send.at[j, 3])
        if j < ITERS:
            left_all(ta_ref.at[j, pl.ds(0, 7)], ar_send.at[j, 4])
    left_all(vc_ref.at[pl.ds(0, 7), 0], mc_send.at[0])
    left_all(vc_ref.at[:, pl.ds(0, 3)], mc_send.at[1])
    left_all(rc_ref, mc_send.at[2])


def local(grm, right_sides, inv_diag, bases, couplings, level_map, variance, iters_per_column):
    order = jnp.concatenate([level_map, jnp.full((1,), 8, jnp.int32)])
    basis = jnp.take(bases.reshape(64, 9, 64), order, axis=1)
    matrices = jnp.take(couplings, order, axis=0)
    basis_t = basis.transpose(1, 2, 0).reshape(576, 64)
    lifted = jnp.einsum("ngr,grs->ngs", basis[:, :8], matrices[:8], precision=HIGHEST).reshape(64, 512)
    coarse = bases[:, 512:]
    coarse_hi = coarse.astype(BF16)
    coarse_lo = (coarse - coarse_hi.astype(F32)).astype(BF16)
    vmem = pl.BlockSpec(memory_space=pltpu.VMEM)
    n = ITERS
    state = pltpu.VMEM((64, 512), F32)
    dma = pltpu.SemaphoreType.DMA
    return pl.pallas_call(
        kernel,
        name="solve",
        out_shape=(jax.ShapeDtypeStruct((64, 512), F32),) * 2,
        in_specs=[pl.BlockSpec(memory_space=pltpu.SMEM), pl.BlockSpec(memory_space=pltpu.HBM)] + [vmem] * 7,
        out_specs=(vmem, vmem),
        scratch_shapes=[
            pltpu.VMEM((8, 64, 2048), BF16),
            pltpu.VMEM((n, 32, 64, 512), BF16),
            pltpu.VMEM((8, 4, 64, 128), BF16),
            pltpu.VMEM((512, 512), F32),
            pltpu.VMEM((n, 8, 64, 512), BF16),
            pltpu.VMEM((n, 8, 64, 512), BF16),
            *[state] * 10,
            pltpu.VMEM((n, 4, 64, 512), BF16),
            pltpu.VMEM((n, 4, 64, 512), BF16),
            pltpu.VMEM((4, 64, 512), F32),
            pltpu.VMEM((n, 3, 64, 512), BF16),
            pltpu.VMEM((n, 3, 64, 512), BF16),
            pltpu.VMEM((8, 64, 128), F32),
            pltpu.VMEM((7, 64, 128), F32),
            pltpu.VMEM((64, 64), F32),
            pltpu.VMEM((64, 64), F32),
            pltpu.VMEM((n + 1, 8, 16, 512), F32),
            pltpu.VMEM((n + 1, 7, 16, 512), F32),
            pltpu.VMEM((n + 1, 4, 16, 128), F32),
            pltpu.VMEM((n + 1, 3, 16, 128), F32),
            pltpu.VMEM((n + 1, 16, 128), F32),
            pltpu.VMEM((n + 1, 7, 16, 128), F32),
            pltpu.VMEM((n + 1, 4, 16, 128), F32),
            pltpu.VMEM((n + 1, 8, 4, 8, 128), F32),
            pltpu.VMEM((8, 512), F32),
            dma((8,)),
            dma((n,)), dma((n, 8)),
            dma((n,)), dma((n, len(GATHER_KEYS))),
            dma((n,)), dma((n,)),
            dma((n,)), dma((n, 3)),
            dma((n + 1, 5)), dma((n + 1, 27)),
            dma((3,)), dma((17,)),
        ],
        compiler_params=pltpu.CompilerParams(
            collective_id=0, has_side_effects=True, vmem_limit_bytes=60 * 1024 * 1024
        ),
    )(
        variance,
        grm.reshape(8, 64, 2048),
        right_sides,
        jnp.broadcast_to(inv_diag[:, None], (64, 128)),
        basis_t,
        lifted,
        jnp.concatenate([coarse_hi, coarse_lo], axis=1),
        couplings[8],
        iters_per_column.reshape(1, 512),
    )


def solution(mesh):
    split = Mesh(mesh.devices.reshape(NY, NC, NZ, NX), HI_LO)
    return jax.shard_map(
        local,
        mesh=split,
        in_specs=(
            P(None, LO, None, HI, None),
            P(HI_LO, None),
            P(HI_LO),
            P(HI_LO, None),
            P(),
            P(),
            P(),
            P(),
        ),
        out_specs=(P(HI_LO, None), P(HI_LO, None)),
        check_vma=False,
    )
```

time: 622 us -> 191 us (0.31); the launches traced: 614 us -> 190 us
  blocking collectives: 293 us -> 0 us
  Pallas kernels: 0 us -> 177 us
  waiting for transfers between devices: 125 us -> 0 us
  matrix products: 73.4 us -> 0.66 us
  starting transfers between devices: 53.4 us -> 0 us
  other arithmetic: 26.7 us -> 2.5 us
  local copies, waits for them, and re-layouts: 27.3 us -> 8.42 us
  between operations: 15.7 us -> 0.72 us
    all_to_all x19 -> x0, blocking collectives: 261 us -> none  [the longest x11 135 us: from_everyone(): return lax.all_to_all(copies, axis, split_axis=0, concat_axis=0, tiled=True)]
    pallas_call x0 -> x1, Pallas kernels: none -> 177 us  [local(): pl.pallas_call(kernel, name='solve', out_shape=(jax.ShapeDtypeStruct((64,...]
    all_gather x3 -> x0, waiting for transfers between devices: 103 us -> none  [gather_axes(): nearer = lax.all_gather(array, axes[-1], axis=dim, tiled=True)]
    dot_general x71 -> x1, matrix products: 73.4 us -> 0.66 us  [local(): jnp.einsum('ngr,grs->ngs', basis[:, :8], matrices[:8], precision=HIGHEST)]
    ppermute x24 -> x0, starting transfers between devices: 40.7 us -> none  [from_partner(): return lax.ppermute(value, axis, pairs)]
    all_gather x3 -> x0, blocking collectives: 31.5 us -> none  [gather_axes(): nearer = lax.all_gather(array, axes[-1], axis=dim, tiled=True)]
    all_to_all x2 -> x0, waiting for transfers between devices: 18.3 us -> none  [the longest x1 14.5 us: sent_and_summed(): lax.all_to_all(tiles, axis, split_axis=0, concat_axis=0, tiled=True)]
    mul x16 -> x0, local copies, waits for them, and re-layouts: 13.7 us -> none  [add_level(): return stacked + select[:, None, None] * term[None]]
  transfers between devices with their start and end apart: 29 -> 0, of which waited for: 9 -> 0; matrix products, arithmetic and copies ran while one was open for 9% -> 0% of each run, Pallas kernels for 0% -> 0%
where the time goes in v1:
time: 191 us; the launch traced here: 190 us
  Pallas kernels  177 us (93%)
  local copies, waits for them, and re-layouts  8.42 us (4%)
  other arithmetic  2.5 us (1%)
    pallas_call x1, Pallas kernels, local(): pl.pallas_call(kernel, name='solve', out_shape=(jax.ShapeDtypeStruct((64,...  177 us
    unnamed x9, local copies, waits for them, and re-layouts  4.21 us

profile of v1, /device:TPU:1, one launch (start us, length us, event | category | flops | bytes accessed | tf_op | source)
XLA Modules:
  0.0 189.8 jit_solution(247604229802732112)
XLA Ops:
  0.6 0.0 copy-start.2
  0.6 0.0 copy-start
  0.6 0.8 fusion.5
  1.4 1.1 copy.13
  2.5 0.1 copy.14
  2.7 0.0 copy-start.1
  2.7 0.6 gather_fusion
  3.2 0.0 copy-done.2
  3.3 0.1 compare_and_fusion
  3.3 0.1 select_bitcast_fusion.1
  3.5 0.0 copy-done
  3.5 0.6 gather_fusion.1
  4.0 0.7 fusion
  4.7 0.8 copy.19.bk_ref
  5.5 0.9 copy.15
  6.3 0.8 subtract_convert_fusion
  7.2 0.7 pad_maximum_fusion.bc_ref
  7.9 0.0 copy-done.1
  7.9 0.7 broadcast_in_dim.26.diag_ref
  8.6 0.6 slice_bitcast_fusion.kc_ref
  9.2 177.5 %solve.1 = (f32[64,512]{1,0:T(8,128)}, f32[64,512]{1,0:T(8,128)}) custom-call(f32[2]{0:T(128)} %var_ref.1, bf16[8,64,2048]{2,1,0:T(8,128)(2,1)} %bitcast.16, f32[64,512]{1,0:T(8,128)} %rhs_ref.1, f32[64,128]{1,0:T(8,128)} %broadcast_in_dim.26.diag_ref, f32[576,64]{1,0:T(8,128)} %bitcast.17, f32[64,512]{1,0:T(8,128)} %copy.19.bk_ref, ...), custom_call_target="tpu_custom_call" | custom-call | tf_op jit(solution)/shard_map/solve/pallas_call | solution.py:489
  186.6 1.6 copy.22
  188.2 1.6 copy.23
  (1 shorter events, 0.0 us)
Async XLA Ops:
  0.6 2.6 %copy-start.2 = (s32[8]{0:T(128)S(1)}, s32[8]{0:T(128)}, u32[]{:S(2)}) copy-start(s32[8]{0:T(128)} %param.13) | copy-start | bytes 100
  0.6 2.8 %copy-start = (f32[9,64,64]{2,1,0:T(8,128)S(1)}, f32[9,64,64]{2,1,0:T(8,128)}, u32[]{:S(2)}) copy-start(f32[9,64,64]{2,1,0:T(8,128)} %param.12) | copy-start | bytes 442372
  2.7 5.2 %copy-start.1 = (f32[64]{0:T(128)S(1)}, f32[64]{0:T(128)}, u32[]{:S(2)}) copy-start(f32[64]{0:T(128)} %param.10) | copy-start | bytes 772
